TPU v7x, 32 devices: a whole 2x2x4 slice. The times are simulated.
32 devices in a mesh: gx: 4 (over y, x), gy: 2 (over core), gz: 4 (over z).
Axes of the slice: x: 2, y: 2, z: 4, core: 2. Of those that a mesh axis runs over, the one named last changes fastest.
Arguments:
- right_side: float32 [64, 128, 1024], P('gx', 'gy', 'gz'), may hold values from -8 to 8
- cell_type: int32 [64, 128, 1024], P('gx', 'gy', 'gz'), may hold values from 0 to 2
- relax_weight: float32 [64, 128, 1024], P('gx', 'gy', 'gz'), may hold values from 0.25 to 2
Outputs:
- pressure: float32 [64, 128, 1024], P('gx', 'gy', 'gz')
- residual: float32 [64, 128, 1024], P('gx', 'gy', 'gz')
Inputs may be any that keep to these rules, and one draw needn't show every extreme that they name: `cell_type`: 0 marks a solid cell, 1 a fluid cell, 2 an empty (air) cell.
All inputs are finite; a program needn't handle non-finite values.
Results may differ from a plain program's by a relative error of at most 0.033.
Values sent between devices are 32-bit elements.
A program may use at most 64 MiB of HBM per device.

v0:
```python
import jax
import jax.numpy as jnp
from jax import lax
from jax.sharding import PartitionSpec as P

ITERS = 8


def extended(cells, sides, width):
    for axis, dim in sides:
        count = lax.axis_size(axis)
        ends = count - 1
        head = lax.slice_in_dim(cells, 0, width, axis=dim)
        tail = lax.slice_in_dim(cells, cells.shape[dim] - width, cells.shape[dim], axis=dim)
        cells = jnp.concatenate(
            [
                lax.ppermute(tail, axis, [(i, (i + 1) % count) for i in range(ends)]),
                cells,
                lax.ppermute(head, axis, [((i + 1) % count, i) for i in range(ends)]),
            ],
            axis=dim,
        )
    return cells


def beside(padded):
    total = padded[2:, 1:-1, 1:-1] + padded[:-2, 1:-1, 1:-1]
    total = total + padded[1:-1, 2:, 1:-1] + padded[1:-1, :-2, 1:-1]
    total = total + padded[1:-1, 1:-1, 2:] + padded[1:-1, 1:-1, :-2]
    return total


def split_limbs(product):
    top = jnp.floor(product * (1.0 / 4096.0))
    rest = product - top * 4096.0
    mid = jnp.floor(rest)
    rest = (rest - mid) * 4096.0
    low = jnp.floor(rest)
    rest = (rest - low) * 4096.0
    least = jnp.floor(rest)
    return [
        least.astype(jnp.int32),
        low.astype(jnp.int32),
        mid.astype(jnp.int32),
        top.astype(jnp.int32),
    ]


def normalize(sums):
    carry = jnp.zeros_like(sums[0])
    limbs_out = []
    for value in sums:
        value = value + carry
        carry = jnp.floor_divide(value, 4096)
        limbs_out.append(value - carry * 4096)
    limbs_out.append(carry)
    return jnp.stack(limbs_out, -1)


def combine(limb_vec):
    parts = limb_vec.astype(jnp.float32)
    total = parts[..., 4] * 16777216.0 + parts[..., 3] * 4096.0
    total = total + parts[..., 2]
    total = total + parts[..., 1] * (1.0 / 4096.0)
    total = total + parts[..., 0] * (1.0 / 16777216.0)
    return total


def local_limbs(first, second):
    limbs = split_limbs(first * second)
    return normalize([jnp.sum(limb, dtype=jnp.int32) for limb in limbs])


def global_sums(limb_rows):
    first = lax.psum(limb_rows, "gx")
    second = lax.psum(first, "gy")
    summed = lax.psum(second, "gz")
    return combine(summed)


def on_device(right_side, cell_type, relax_weight):
    padded_type = extended(cell_type, (("gx", 0), ("gy", 1), ("gz", 2)), 1)
    open_count = beside((padded_type != 0).astype(jnp.float32))
    fluid_cell = (cell_type == 1).astype(jnp.float32)
    weight = fluid_cell * (relax_weight + open_count)
    pressure = jnp.zeros_like(right_side)
    residual = fluid_cell * right_side
    direction = residual
    norm_now = global_sums(local_limbs(residual, residual)[None, :])[0]
    for iteration in range(ITERS):
        padded = extended(direction, (("gx", 0), ("gy", 1), ("gz", 2)), 1)
        image_field = weight * direction - fluid_cell * beside(padded)
        curve = global_sums(local_limbs(direction, image_field)[None, :])[0]
        step_size = norm_now / curve
        pressure = pressure + step_size * direction
        residual = residual - step_size * image_field
        norm_next = global_sums(local_limbs(residual, residual)[None, :])[0]
        direction = residual + norm_next / norm_now * direction
        norm_now = norm_next
    return (pressure, residual)


def solution(mesh):
    return jax.shard_map(
        on_device,
        mesh=mesh,
        in_specs=(P("gx", "gy", "gz"), P("gx", "gy", "gz"), P("gx", "gy", "gz")),
        out_specs=(P("gx", "gy", "gz"), P("gx", "gy", "gz")),
        check_vma=False,
    )
```

profile of v0, /device:TPU:0, one launch (start us, length us, event | category | flops | bytes accessed | tf_op | source)
XLA Modules:
  0.0 770.5 jit_solution(10256962476088027891)
XLA Ops:
  1.5 4.9 collective-permute-start
  17.0 4.3 collective-permute-start.7
  23.2 4.3 collective-permute-done.6
  29.4 4.2 collective-permute-start.9
  53.6 4.6 collective-permute-start.11
  66.1 9.1 %fusion.185 = (f32[16,64,256]{2,1,0:T(8,128)S(1)}, f32[16,64,256]{2,1,0:T(8,128)S(1)}, f32[16,64,256]{2,1,0:T(8,128)S(1)}) fusion(f32[16,64,256]{2,1,0:T(8,128)S(1)} %get-tuple-element.102, pred[16,64,256]{2,1,0:T(8,128)(4,1)S(1)} %get-tuple-element.103, f32[18,1,256]{2,1,0:T(1,128)} %copy-done.23, f32[1,64,256]{2,1,0:T(8,128)S(1)} %collective-permute-done.6, ...), kind=kLoop, calls=%fused_computation.494 | loop fusion | flops 8912896 | bytes 11973920 | tf_op jit(solution)/shard_map/mul | solution.py:70
  82.5 6.4 all-reduce.1
  90.6 8.5 %all-reduce = (s32[1,5]{1,0:T(1,128)S(1)}, s32[1,5]{1,0:T(1,128)S(1)}) all-reduce(s32[1,5]{1,0:T(1,128)S(1)} %get-tuple-element.76, s32[1,5]{1,0:T(1,128)S(1)} %get-tuple-element.77), channel_id=1, replica_groups=mesh['gx'=4,'gy'=2,'gz'=4] {'gz'}, use_global_device_ids=true, to_apply=%region_6.7 | all-reduce | flops 10 | bytes 80 | tf_op jit(solution)/shard_map/psum | solution.py:77
  114.3 7.6 psum.342
  123.8 6.1 psum.344
  141.0 4.3 collective-permute-done.12
  157.2 5.1 collective-permute-start.17
  166.1 4.9 fusion.183
  177.7 5.6 psum.345
  185.1 8.6 %psum.347 = s32[1,5]{1,0:T(1,128)S(1)} all-reduce(s32[1,5]{1,0:T(1,128)S(1)} %psum.346), channel_id=1, replica_groups=mesh['gx'=4,'gy'=2,'gz'=4] {'gz'}, use_global_device_ids=true, to_apply=%region_27.28 | all-reduce | flops 5 | bytes 40 | tf_op jit(solution)/shard_map/psum | solution.py:77
  197.5 4.1 convert_reduce_fusion.11
  206.9 8.1 %psum.348 = s32[1,5]{1,0:T(1,128)S(1)} all-reduce(s32[1,5]{1,0:T(1,128)S(1)} %bitcast.115), channel_id=1, replica_groups=mesh['gx'=4,'gy'=2,'gz'=4] {'gx'}, use_global_device_ids=true, to_apply=%region_32.33 | all-reduce | flops 5 | bytes 40 | tf_op jit(solution)/shard_map/psum | solution.py:75
  216.8 6.0 psum.350
  232.9 4.3 collective-permute-done.18
  248.6 5.1 collective-permute-start.23
  257.5 7.8 %fusion.181 = (f32[16,64,256]{2,1,0:T(8,128)S(1)}, f32[16,64,256]{2,1,0:T(8,128)}) fusion(f32[16,64,256]{2,1,0:T(8,128)} %copy-done, pred[16,64,256]{2,1,0:T(8,128)(4,1)S(1)} %get-tuple-element.103, f32[18,1,256]{2,1,0:T(1,128)} %copy-done.11, f32[1,64,256]{2,1,0:T(8,128)S(1)} %collective-permute-done.18, f32[1,64,256]{2,1,0:T(8,128)S(1)} %collective-permute-done.19, ...), kind=kLoop, calls=%fused_computation.492 | loop fusion | flops 7077888 | bytes 4633888 | tf_op jit(solution)/shard_map/mul | solution.py:70
  272.0 5.6 psum.351
  279.4 8.8 %psum.353 = s32[1,5]{1,0:T(1,128)S(1)} all-reduce(s32[1,5]{1,0:T(1,128)S(1)} %psum.352), channel_id=1, replica_groups=mesh['gx'=4,'gy'=2,'gz'=4] {'gz'}, use_global_device_ids=true, to_apply=%region_41.42 | all-reduce | flops 5 | bytes 40 | tf_op jit(solution)/shard_map/psum | solution.py:77
  291.9 4.1 convert_reduce_fusion.9
  301.5 8.1 %psum.354 = s32[1,5]{1,0:T(1,128)S(1)} all-reduce(s32[1,5]{1,0:T(1,128)S(1)} %bitcast.117), channel_id=1, replica_groups=mesh['gx'=4,'gy'=2,'gz'=4] {'gx'}, use_global_device_ids=true, to_apply=%region_46.47 | all-reduce | flops 5 | bytes 40 | tf_op jit(solution)/shard_map/psum | solution.py:75
  311.5 6.0 psum.356
  328.1 4.3 collective-permute-done.24
  343.8 5.1 collective-permute-start.29
  352.7 7.4 fusion.179
  366.8 5.6 psum.357
  374.2 8.9 %psum.359 = s32[1,5]{1,0:T(1,128)S(1)} all-reduce(s32[1,5]{1,0:T(1,128)S(1)} %psum.358), channel_id=1, replica_groups=mesh['gx'=4,'gy'=2,'gz'=4] {'gz'}, use_global_device_ids=true, to_apply=%region_55.56 | all-reduce | flops 5 | bytes 40 | tf_op jit(solution)/shard_map/psum | solution.py:77
  386.8 4.1 convert_reduce_fusion.7
  395.9 8.1 %psum.360 = s32[1,5]{1,0:T(1,128)S(1)} all-reduce(s32[1,5]{1,0:T(1,128)S(1)} %bitcast.119), channel_id=1, replica_groups=mesh['gx'=4,'gy'=2,'gz'=4] {'gx'}, use_global_device_ids=true, to_apply=%region_60.61 | all-reduce | flops 5 | bytes 40 | tf_op jit(solution)/shard_map/psum | solution.py:75
  405.8 5.8 psum.362
  421.9 4.3 collective-permute-done.30
  437.6 5.1 collective-permute-start.35
  446.5 7.3 fusion.177
  460.7 5.6 psum.363
  468.1 9.2 %psum.365 = s32[1,5]{1,0:T(1,128)S(1)} all-reduce(s32[1,5]{1,0:T(1,128)S(1)} %psum.364), channel_id=1, replica_groups=mesh['gx'=4,'gy'=2,'gz'=4] {'gz'}, use_global_device_ids=true, to_apply=%region_69.70 | all-reduce | flops 5 | bytes 40 | tf_op jit(solution)/shard_map/psum | solution.py:77
  480.9 4.1 convert_reduce_fusion.5
  489.8 8.1 %psum.366 = s32[1,5]{1,0:T(1,128)S(1)} all-reduce(s32[1,5]{1,0:T(1,128)S(1)} %bitcast.121), channel_id=1, replica_groups=mesh['gx'=4,'gy'=2,'gz'=4] {'gx'}, use_global_device_ids=true, to_apply=%region_74.75 | all-reduce | flops 5 | bytes 40 | tf_op jit(solution)/shard_map/psum | solution.py:75
  499.8 5.6 psum.368
  515.9 4.3 collective-permute-done.36
  531.6 5.1 collective-permute-start.41
  540.5 7.3 fusion.175
  554.6 5.6 psum.369
  562.1 9.1 %psum.371 = s32[1,5]{1,0:T(1,128)S(1)} all-reduce(s32[1,5]{1,0:T(1,128)S(1)} %psum.370), channel_id=1, replica_groups=mesh['gx'=4,'gy'=2,'gz'=4] {'gz'}, use_global_device_ids=true, to_apply=%region_83.84 | all-reduce | flops 5 | bytes 40 | tf_op jit(solution)/shard_map/psum | solution.py:77
  574.9 4.1 convert_reduce_fusion.3
  584.1 8.1 %psum.372 = s32[1,5]{1,0:T(1,128)S(1)} all-reduce(s32[1,5]{1,0:T(1,128)S(1)} %bitcast.123), channel_id=1, replica_groups=mesh['gx'=4,'gy'=2,'gz'=4] {'gx'}, use_global_device_ids=true, to_apply=%region_88.89 | all-reduce | flops 5 | bytes 40 | tf_op jit(solution)/shard_map/psum | solution.py:75
  594.1 5.6 psum.374
  609.8 4.3 collective-permute-done.42
  625.6 5.4 collective-permute-start.47
  634.7 7.6 fusion.173
  649.3 5.6 psum.375
  656.7 9.1 %psum.377 = s32[1,5]{1,0:T(1,128)S(1)} all-reduce(s32[1,5]{1,0:T(1,128)S(1)} %psum.376), channel_id=1, replica_groups=mesh['gx'=4,'gy'=2,'gz'=4] {'gz'}, use_global_device_ids=true, to_apply=%region_97.98 | all-reduce | flops 5 | bytes 40 | tf_op jit(solution)/shard_map/psum | solution.py:77
  669.6 4.1 convert_reduce_fusion.1
  679.0 8.1 %psum.378 = s32[1,5]{1,0:T(1,128)S(1)} all-reduce(s32[1,5]{1,0:T(1,128)S(1)} %bitcast.125), channel_id=1, replica_groups=mesh['gx'=4,'gy'=2,'gz'=4] {'gx'}, use_global_device_ids=true, to_apply=%region_102.103 | all-reduce | flops 5 | bytes 40 | tf_op jit(solution)/shard_map/psum | solution.py:75
  688.9 5.6 psum.380
  705.0 4.3 collective-permute-done.48
  720.8 5.1 collective-permute-start.53
  729.7 7.4 fusion.171
  744.1 5.6 psum.381
  751.5 9.1 %psum.383 = s32[1,5]{1,0:T(1,128)S(1)} all-reduce(s32[1,5]{1,0:T(1,128)S(1)} %psum.382), channel_id=1, replica_groups=mesh['gx'=4,'gy'=2,'gz'=4] {'gz'}, use_global_device_ids=true, to_apply=%region_111.112 | all-reduce | flops 5 | bytes 40 | tf_op jit(solution)/shard_map/psum | solution.py:77
  764.3 5.8 multiply_subtract_fusion
  (330 shorter events, 246.6 us)
Async XLA Ops:
  1.5 6.8 collective-permute-start
  6.4 6.2 collective-permute-start.1
  12.6 10.2 %copy-start.7 = (s32[18,64,256]{2,1,0:T(8,128)}, s32[18,64,256]{2,1,0:T(8,128)S(1)}, u32[]{:S(2)}) copy-start(s32[18,64,256]{2,1,0:T(8,128)S(1)} %constant_dynamic-update-slice_fusion) | copy-start | bytes 3538948
  12.6 10.0 %collective-permute-start.3 = (s32[18,1,256]{2,0,1:T(8,128)S(1)}, s32[18,1,256]{2,0,1:T(8,128)S(1)}, u32[]{:S(2)}, u32[]{:S(2)}) collective-permute-start(s32[18,1,256]{2,0,1:T(8,128)S(1)} %copy.434), channel_id=1, source_target_pairs={{4,0},{5,1},{6,2},{7,3},{12,8},{13,9},{14,10},{15,11},{20,16},{21,... | collective-permute-start | bytes 55304 | tf_op jit(solution)/shard_map/ppermute | solution.py:19
  13.9 8.7 %collective-permute-start.2 = (s32[18,1,256]{2,0,1:T(8,128)S(1)}, s32[18,1,256]{2,0,1:T(8,128)S(1)}, u32[]{:S(2)}, u32[]{:S(2)}) collective-permute-start(s32[18,1,256]{2,0,1:T(8,128)S(1)} %copy.433), channel_id=1, source_target_pairs={{0,4},{1,5},{2,6},{3,7},{8,12},{9,13},{10,14},{11,15},{16,20},{17,... | collective-permute-start | bytes 55304 | tf_op jit(solution)/shard_map/ppermute | solution.py:17
  17.0 6.2 collective-permute-start.7
  21.3 6.2 collective-permute-start.6
  28.1 19.6 %collective-permute-start.8 = (f32[18,1,256]{2,0,1:T(8,128)}, f32[18,1,256]{2,0,1:T(8,128)}, u32[]{:S(2)}, u32[]{:S(2)}) collective-permute-start(f32[18,1,256]{2,0,1:T(8,128)} %copy.353), channel_id=1, source_target_pairs={{4,0},{5,1},{6,2},{7,3},{12,8},{13,9},{14,10},{15,11},{20,16},{21,... | collective-permute-start | bytes 55304 | tf_op jit(solution)/shard_map/ppermute | solution.py:19
  29.4 19.1 %collective-permute-start.9 = (f32[18,1,256]{2,0,1:T(8,128)S(1)}, f32[18,1,256]{2,0,1:T(8,128)}, u32[]{:S(2)}, u32[]{:S(2)}) collective-permute-start(f32[18,1,256]{2,0,1:T(8,128)S(1)} %copy.355), channel_id=1, source_target_pairs={{0,4},{1,5},{2,6},{3,7},{8,12},{9,13},{10,14},{11,15},{16,20},{17,... | collective-permute-start | bytes 55304 | tf_op jit(solution)/shard_map/ppermute | solution.py:17
  36.1 10.1 %collective-permute-start.4 = (s32[18,66,1]{1,0,2:T(8,128)S(1)}, s32[18,66,1]{1,0,2:T(8,128)S(1)}, u32[]{:S(2)}, u32[]{:S(2)}) collective-permute-start(s32[18,66,1]{1,0,2:T(8,128)S(1)} %copy.349), channel_id=1, source_target_pairs={{0,1},{1,2},{2,3},{4,5},{5,6},{6,7},{8,9},{9,10},{10,11},{12,13},{... | collective-permute-start | bytes 14264 | tf_op jit(solution)/shard_map/ppermute | solution.py:17
  39.9 6.6 collective-permute-start.5
  50.7 8.8 %copy-start.8 = (s32[18,64,256]{2,1,0:T(8,128)S(1)}, s32[18,64,256]{2,1,0:T(8,128)}, u32[]{:S(2)}) copy-start(s32[18,64,256]{2,1,0:T(8,128)} %copy-done.7) | copy-start | bytes 3538948
  53.6 11.3 %collective-permute-start.11 = (f32[18,66,1]{1,0,2:T(8,128)S(1)}, f32[18,66,1]{1,0,2:T(8,128)S(1)}, u32[]{:S(2)}, u32[]{:S(2)}) collective-permute-start(f32[18,66,1]{1,0,2:T(8,128)S(1)} %copy.361), channel_id=1, source_target_pairs={{0,1},{1,2},{2,3},{4,5},{5,6},{6,7},{8,9},{9,10},{10,11},{12,13},{... | collective-permute-start | bytes 14264 | tf_op jit(solution)/shard_map/ppermute | solution.py:17
  58.2 5.6 collective-permute-start.10
  135.2 5.8 collective-permute-start.13
  139.1 6.2 collective-permute-start.12
  145.3 4.4 collective-permute-start.14
  146.6 3.9 collective-permute-start.15
  153.4 8.9 %collective-permute-start.16 = (f32[18,66,1]{1,0,2:T(8,128)S(1)}, f32[18,66,1]{1,0,2:T(8,128)}, u32[]{:S(2)}, u32[]{:S(2)}) collective-permute-start(f32[18,66,1]{1,0,2:T(8,128)S(1)} %copy.369), channel_id=1, source_target_pairs={{1,0},{2,1},{3,2},{5,4},{6,5},{7,6},{9,8},{10,9},{11,10},{13,12},{... | collective-permute-start | bytes 14264 | tf_op jit(solution)/shard_map/ppermute | solution.py:19
  157.2 7.0 collective-permute-start.17
  228.1 14.5 %copy-start = (f32[16,64,256]{2,1,0:T(8,128)}, f32[16,64,256]{2,1,0:T(8,128)S(1)}, u32[]{:S(2)}) copy-start(f32[16,64,256]{2,1,0:T(8,128)S(1)} %multiply_add_fusion.6) | copy-start | bytes 3145732
  228.1 4.7 collective-permute-start.19
  231.0 6.2 collective-permute-start.18
  237.2 4.4 collective-permute-start.20
  238.5 3.9 collective-permute-start.21
  245.2 8.5 %collective-permute-start.22 = (f32[18,66,1]{1,0,2:T(8,128)S(1)}, f32[18,66,1]{1,0,2:T(8,128)}, u32[]{:S(2)}, u32[]{:S(2)}) collective-permute-start(f32[18,66,1]{1,0,2:T(8,128)S(1)} %copy.379), channel_id=1, source_target_pairs={{1,0},{2,1},{3,2},{5,4},{6,5},{7,6},{9,8},{10,9},{11,10},{13,12},{... | collective-permute-start | bytes 14264 | tf_op jit(solution)/shard_map/ppermute | solution.py:19
  248.6 7.0 collective-permute-start.23
  323.0 14.7 %copy-start.2 = (f32[16,64,256]{2,1,0:T(8,128)}, f32[16,64,256]{2,1,0:T(8,128)S(1)}, u32[]{:S(2)}) copy-start(f32[16,64,256]{2,1,0:T(8,128)S(1)} %multiply_add_fusion.5) | copy-start | bytes 3145732
  323.1 5.0 collective-permute-start.25
  326.2 6.2 collective-permute-start.24
  332.4 4.4 collective-permute-start.26
  333.7 3.9 collective-permute-start.27
  340.5 8.5 %collective-permute-start.28 = (f32[18,66,1]{1,0,2:T(8,128)S(1)}, f32[18,66,1]{1,0,2:T(8,128)}, u32[]{:S(2)}, u32[]{:S(2)}) collective-permute-start(f32[18,66,1]{1,0,2:T(8,128)S(1)} %copy.389), channel_id=1, source_target_pairs={{1,0},{2,1},{3,2},{5,4},{6,5},{7,6},{9,8},{10,9},{11,10},{13,12},{... | collective-permute-start | bytes 14264 | tf_op jit(solution)/shard_map/ppermute | solution.py:19
  343.8 7.0 collective-permute-start.29
  417.1 14.5 %copy-start.3 = (f32[16,64,256]{2,1,0:T(8,128)}, f32[16,64,256]{2,1,0:T(8,128)S(1)}, u32[]{:S(2)}) copy-start(f32[16,64,256]{2,1,0:T(8,128)S(1)} %multiply_add_fusion.4) | copy-start | bytes 3145732
  417.1 4.7 collective-permute-start.31
  420.0 6.2 collective-permute-start.30
  426.2 4.4 collective-permute-start.32
  427.5 3.9 collective-permute-start.33
  430.6 2.3 copy-start.13
  434.3 8.5 %collective-permute-start.34 = (f32[18,66,1]{1,0,2:T(8,128)S(1)}, f32[18,66,1]{1,0,2:T(8,128)}, u32[]{:S(2)}, u32[]{:S(2)}) collective-permute-start(f32[18,66,1]{1,0,2:T(8,128)S(1)} %copy.399), channel_id=1, source_target_pairs={{1,0},{2,1},{3,2},{5,4},{6,5},{7,6},{9,8},{10,9},{11,10},{13,12},{... | collective-permute-start | bytes 14264 | tf_op jit(solution)/shard_map/ppermute | solution.py:19
  437.6 7.0 collective-permute-start.35
  510.8 14.7 %copy-start.4 = (f32[16,64,256]{2,1,0:T(8,128)}, f32[16,64,256]{2,1,0:T(8,128)S(1)}, u32[]{:S(2)}) copy-start(f32[16,64,256]{2,1,0:T(8,128)S(1)} %multiply_add_fusion.3) | copy-start | bytes 3145732
  510.9 5.0 collective-permute-start.37
  514.0 6.2 collective-permute-start.36
  520.2 4.4 collective-permute-start.38
  521.5 3.9 collective-permute-start.39
  528.3 8.5 %collective-permute-start.40 = (f32[18,66,1]{1,0,2:T(8,128)S(1)}, f32[18,66,1]{1,0,2:T(8,128)}, u32[]{:S(2)}, u32[]{:S(2)}) collective-permute-start(f32[18,66,1]{1,0,2:T(8,128)S(1)} %copy.409), channel_id=1, source_target_pairs={{1,0},{2,1},{3,2},{5,4},{6,5},{7,6},{9,8},{10,9},{11,10},{13,12},{... | collective-permute-start | bytes 14264 | tf_op jit(solution)/shard_map/ppermute | solution.py:19
  531.6 7.0 collective-permute-start.41
  605.1 14.5 %copy-start.5 = (f32[16,64,256]{2,1,0:T(8,128)}, f32[16,64,256]{2,1,0:T(8,128)S(1)}, u32[]{:S(2)}) copy-start(f32[16,64,256]{2,1,0:T(8,128)S(1)} %multiply_add_fusion.2) | copy-start | bytes 3145732
  605.1 4.7 collective-permute-start.43
  608.0 6.2 collective-permute-start.42
  614.2 4.4 collective-permute-start.44
  615.5 3.9 collective-permute-start.45
  622.2 8.7 %collective-permute-start.46 = (f32[18,66,1]{1,0,2:T(8,128)S(1)}, f32[18,66,1]{1,0,2:T(8,128)}, u32[]{:S(2)}, u32[]{:S(2)}) collective-permute-start(f32[18,66,1]{1,0,2:T(8,128)S(1)} %copy.419), channel_id=1, source_target_pairs={{1,0},{2,1},{3,2},{5,4},{6,5},{7,6},{9,8},{10,9},{11,10},{13,12},{... | collective-permute-start | bytes 14264 | tf_op jit(solution)/shard_map/ppermute | solution.py:19
  625.6 7.3 collective-permute-start.47
  700.0 14.7 %copy-start.6 = (f32[16,64,256]{2,1,0:T(8,128)}, f32[16,64,256]{2,1,0:T(8,128)S(1)}, u32[]{:S(2)}) copy-start(f32[16,64,256]{2,1,0:T(8,128)S(1)} %multiply_add_fusion.1) | copy-start | bytes 3145732
  700.0 5.0 collective-permute-start.49
  703.2 6.2 collective-permute-start.48
  709.4 4.4 collective-permute-start.50
  710.7 3.9 collective-permute-start.51
  717.4 8.5 %collective-permute-start.52 = (f32[18,66,1]{1,0,2:T(8,128)S(1)}, f32[18,66,1]{1,0,2:T(8,128)}, u32[]{:S(2)}, u32[]{:S(2)}) collective-permute-start(f32[18,66,1]{1,0,2:T(8,128)S(1)} %copy.429), channel_id=1, source_target_pairs={{1,0},{2,1},{3,2},{5,4},{6,5},{7,6},{9,8},{10,9},{11,10},{13,12},{... | collective-permute-start | bytes 14264 | tf_op jit(solution)/shard_map/ppermute | solution.py:19
  720.8 7.0 collective-permute-start.53
  737.1 27.2 %copy-start.1 = (f32[16,64,256]{2,1,0:T(8,128)S(1)}, f32[16,64,256]{2,1,0:T(8,128)}, u32[]{:S(2)}) copy-start(f32[16,64,256]{2,1,0:T(8,128)} %copy-done) | copy-start | bytes 3145732
  (15 other events, 27.7 us)
where the time goes:
time: 784 us; the launch traced here: 771 us
  blocking collectives  241 us (31%)
  starting transfers between devices  139 us (18%)
  between operations  133 us (17%)
  other arithmetic  125 us (16%)
  local copies, waits for them, and re-layouts  85.7 us (11%)
  waiting for transfers between devices  46.8 us (6%)
    psum x15, blocking collectives, global_sums(): summed = lax.psum(second, 'gz')  112 us
    ppermute x27, starting transfers between devices, extended(): lax.ppermute(tail, axis, [(i, (i + 1) % count) for i in range(ends)])  104 us
    psum x15, blocking collectives, global_sums(): first = lax.psum(limb_rows, 'gx')  102 us
    mul x8, other arithmetic, local_limbs(): limbs = split_limbs(first * second)  58.9 us
    reduce_sum x16, other arithmetic, local_limbs(): return normalize([jnp.sum(limb, dtype=jnp.int32) for limb in limbs])  44.6 us
    ppermute x27, waiting for transfers between devices, extended(): lax.ppermute(head, axis, [((i + 1) % count, i) for i in range(ends)])  36.2 us
    ppermute x27, starting transfers between devices, extended(): lax.ppermute(head, axis, [((i + 1) % count, i) for i in range(ends)])  35.4 us
    psum x15, blocking collectives, global_sums(): second = lax.psum(first, 'gy')  27.2 us
  transfers between devices with their start and end apart: 54, of which 26 were waited for; matrix products, arithmetic and copies ran while one was open for 5% of the time, Pallas kernels for 0%

commit v1 on v0

v1 whole, which is shorter than its diff:
```python
import functools

import jax
import jax.numpy as jnp
from jax import lax
from jax.experimental import pallas as pl
from jax.experimental.pallas import tpu as pltpu
from jax.sharding import PartitionSpec as P

ITERS = 8
AXES = ("gx", "gy", "gz")
MESH = pl.DeviceIdType.MESH
LANES = 128
ROWS = 8
OPEN, START = 2, 3


def kernel(counts, rhs, kind, relax, pressure, residual, ext, hy, hz, sy, sz, p, s, z, n, weight, fluid,
           mine, others, hsend, hrecv, asend, arecv):
    cx, cy, cz = rhs.shape
    tiles = cy // ROWS
    me = tuple(lax.axis_index(a) for a in AXES)
    lane = lax.broadcasted_iota(jnp.int32, (ROWS, LANES), 1)
    row_of = lax.broadcasted_iota(jnp.int32, (cy, cz), 0)
    col_of = lax.broadcasted_iota(jnp.int32, (cy, cz), 1)

    offsets = [(a, b, c) for a in range(counts[0]) for b in range(counts[1]) for c in range(counts[2])][1:]
    offsets.sort(key=lambda o: -sum(min(v, m - v) for v, m in zip(o, counts)))
    my_row = (me[0] * counts[1] + me[1]) * counts[2] + me[2]

    def peer(o):
        return tuple(lax.rem(m + v, c) if v else m for m, v, c in zip(me, o, counts))

    barrier = pltpu.get_barrier_semaphore()

    def halo(b, axis, up):
        target = tuple(m + (1 if up else -1) if d == axis else m for d, m in enumerate(me))
        if axis == 0:
            src, dst = (ext.at[b, cx], ext.at[b, 0]) if up else (ext.at[b, 1], ext.at[b, cx + 1])
        elif axis == 1:
            src, dst = sy.at[b, 1 if up else 0], hy.at[b, 0 if up else 1]
        else:
            src, dst = sz.at[b, 1 if up else 0], hz.at[b, 0 if up else 1]
        where = 2 * axis + (0 if up else 1)
        return pltpu.make_async_remote_copy(
            src_ref=src, dst_ref=dst, send_sem=hsend.at[b, where], recv_sem=hrecv.at[b, where],
            device_id=target, device_id_type=MESH)

    def halo_do(b, axes, what):
        for axis in axes:
            if counts[axis] == 1:
                continue
            for up in (True, False):
                leaves = me[axis] < counts[axis] - 1 if up else me[axis] > 0
                reaches = me[axis] > 0 if up else me[axis] < counts[axis] - 1

                @pl.when(reaches if what == "recv" else leaves)
                def _():
                    copy = halo(b, axis, up)
                    if what == "start":
                        copy.start()
                    elif what == "recv":
                        copy.wait_recv()
                    else:
                        copy.wait_send()

    def pack_faces(b, x, value, packed):
        sy[b, 0, pl.ds(x, 1), :] = value[:1, :]
        sy[b, 1, pl.ds(x, 1), :] = value[cy - 1:, :]
        low, high = packed
        for t in range(tiles):
            q = t * cx + x
            rows = value[t * ROWS:(t + 1) * ROWS]
            low = jnp.where(lane == q, pltpu.roll(rows[:, :LANES], q, 1), low)
            high = jnp.where(lane == q, pltpu.roll(rows[:, cz - LANES:], lax.rem(q + 1, LANES), 1), high)
        return low, high

    def neighbours(b, x):
        centre = ext[b, x + 1]
        total = ext[b, x] + ext[b, x + 2]
        before = jnp.where(row_of == 0, hy[b, 0, pl.ds(x, 1), :], pltpu.roll(centre, 1, 0))
        after = jnp.where(row_of == cy - 1, hy[b, 1, pl.ds(x, 1), :], pltpu.roll(centre, cy - 1, 0))
        total = total + before + after
        first, last = hz[b, 0], hz[b, 1]
        lows = [pltpu.roll(first, lax.rem(LANES - (t * cx + x), LANES), 1) for t in range(tiles)]
        highs = [pltpu.roll(last, LANES - 1 - (t * cx + x), 1) for t in range(tiles)]
        reps = cz // LANES
        low = jnp.concatenate([jnp.concatenate(lows, 0)] * reps, 1)
        high = jnp.concatenate([jnp.concatenate(highs, 0)] * reps, 1)
        before = jnp.where(col_of == 0, low, pltpu.roll(centre, 1, 1))
        after = jnp.where(col_of == cz - 1, high, pltpu.roll(centre, cz - 1, 1))
        return centre, total + before + after

    def add_limbs(product, acc):
        whole = jnp.floor(product)
        frac = ((product - whole) * 16777216.0).astype(jnp.int32)
        whole = whole.astype(jnp.int32)

        def fold(v):
            parts = [v[i:i + ROWS, j:j + LANES] for i in range(0, v.shape[0], ROWS) for j in range(0, cz, LANES)]
            while len(parts) > 1:
                parts = [a + c for a, c in zip(parts[::2], parts[1::2])]
            return parts[0]

        frac, whole = fold(frac), fold(whole)
        a0, a1, a2, a3 = acc
        return (a0 + (frac & 4095), a1 + (frac >> 12), a2 + (whole & 4095), a3 + (whole >> 12))

    def ring_copy(k, i, o):
        return pltpu.make_async_remote_copy(
            src_ref=mine.at[k], dst_ref=others.at[k, pl.ds(my_row, 1)], send_sem=asend.at[k, i],
            recv_sem=arecv.at[k, i], device_id=peer(o), device_id_type=MESH)

    def send_sums(k, dots):
        rows = []
        for acc in dots:
            carry = None
            for level, v in enumerate(acc):
                v = v if carry is None else v + carry
                if level < 3:
                    carry = v >> 12
                    v = v & 4095
                rows.append(jnp.sum(v, axis=0, keepdims=True))
        block = jnp.concatenate(rows, 0)
        for shift in (64, 32, 16, 8, 4, 2, 1):
            block = block + pltpu.roll(block, shift, 1)
        diag = lane == lax.broadcasted_iota(jnp.int32, (ROWS, LANES), 0)
        mine[k] = jnp.sum(jnp.where(diag, block, 0), axis=0, keepdims=True)
        for i, o in enumerate(offsets):
            ring_copy(k, i, o).start()

    def wait_sums(k):
        for i, o in enumerate(offsets):
            ring_copy(k, i, o).wait_recv()
        total = jnp.sum(others[k], axis=0, keepdims=True) + mine[k]
        total = jnp.broadcast_to(total, (ROWS, LANES))
        level = lane & 3
        for _ in range(3):
            carry = jnp.where(level == 3, 0, total >> 12)
            total = jnp.where(level == 3, total, total & 4095) + pltpu.roll(carry, 1, 1)
        scale = jnp.where(level == 0, 1.0 / 16777216.0,
                          jnp.where(level == 1, 1.0 / 4096.0, jnp.where(level == 2, 1.0, 4096.0)))
        value = total.astype(jnp.float32) * scale
        value = value + pltpu.roll(value, LANES - 1, 1)
        value = value + pltpu.roll(value, LANES - 2, 1)
        return value[:1, 0:1], value[:1, 4:5]

    def done_sums(k):
        for i, o in enumerate(offsets):
            ring_copy(k, i, o).wait_send()

    def steps(gamma, delta, gamma_old, alpha_old):
        beta = gamma / gamma_old
        alpha = gamma / (delta - beta * gamma / alpha_old)
        return alpha, beta

    no_sums = tuple(jnp.zeros((ROWS, LANES), jnp.int32) for _ in range(4))
    no_faces = (jnp.zeros((ROWS, LANES), jnp.float32),) * 2

    edge = jnp.zeros((cy, cz), jnp.float32)
    for b in range(4):
        ext[b, 0] = edge
        ext[b, cx + 1] = edge
    hy[...] = jnp.zeros_like(hy)
    hz[...] = jnp.zeros_like(hz)
    others[...] = jnp.zeros_like(others)
    for o in offsets:
        pl.semaphore_signal(barrier, inc=1, device_id=peer(o), device_id_type=MESH)

    def first(x, carry):
        packed_open, packed_start = carry
        types = kind[x]
        is_fluid = jnp.where(types == 1, 1.0, 0.0)
        is_open = jnp.where(types != 0, 1.0, 0.0)
        start = is_fluid * rhs[x]
        fluid[x] = is_fluid
        ext[OPEN, x + 1] = is_open
        ext[START, x + 1] = start
        return pack_faces(OPEN, x, is_open, packed_open), pack_faces(START, x, start, packed_start)

    packed_open, packed_start = lax.fori_loop(0, cx, first, (no_faces, no_faces))
    for b, packed in ((OPEN, packed_open), (START, packed_start)):
        sz[b, 0], sz[b, 1] = packed
    pl.semaphore_wait(barrier, len(offsets))
    for b in (OPEN, START):
        halo_do(b, (0, 1, 2), "start")

    def clear(x, carry):
        for ref in (p, s, z, pressure):
            ref[x] = edge
        return carry

    lax.fori_loop(0, cx, clear, 0)
    for b in (OPEN, START):
        halo_do(b, (1, 2), "recv")

    def begin(x, carry):
        packed, norms, curves = carry
        _, count = neighbours(OPEN, x)
        weighed = fluid[x] * (relax[x] + count)
        weight[x] = weighed
        start, around = neighbours(START, x)
        image = weighed * start - fluid[x] * around
        ext[0, x + 1] = image
        return (pack_faces(0, x, image, packed), add_limbs(start * start, norms), add_limbs(start * image, curves))

    carry = lax.fori_loop(1, cx - 1, begin, (no_faces, no_sums, no_sums))
    for b in (OPEN, START):
        halo_do(b, (0,), "recv")
    carry = lax.fori_loop(0, 2, lambda i, c: begin(i * (cx - 1), c), carry)
    sz[0, 0], sz[0, 1] = carry[0]
    halo_do(0, (0, 1, 2), "start")
    send_sums(0, carry[1:])

    def apply(b):
        def one(x, carry):
            centre, around = neighbours(b, x)
            n[x] = weight[x] * centre - fluid[x] * around
            return carry

        halo_do(b, (1, 2), "recv")
        lax.fori_loop(1, cx - 1, one, 0)
        halo_do(b, (0,), "recv")
        lax.fori_loop(0, 2, lambda i, c: one(i * (cx - 1), c), 0)

    apply(0)
    for b in (OPEN, START):
        halo_do(b, (0, 1, 2), "send")

    def iteration(k, carry):
        b = lax.rem(k, 2)
        c = 1 - b
        gamma, delta = wait_sums(b)
        alpha, beta = steps(gamma, delta, *carry)
        halo_do(b, (0, 1, 2), "send")
        done_sums(b)

        def update(x, carry):
            packed, norms, curves = carry
            old = ext[b, x + 1]
            z_new = n[x] + beta * z[x]
            z[x] = z_new
            w_new = old - alpha * z_new
            ext[c, x + 1] = w_new
            s_new = old + beta * s[x]
            s[x] = s_new
            r_old = ext[START, x + 1]
            p_new = r_old + beta * p[x]
            p[x] = p_new
            pressure[x] = pressure[x] + alpha * p_new
            r_new = r_old - alpha * s_new
            ext[START, x + 1] = r_new
            return (pack_faces(c, x, w_new, packed), add_limbs(r_new * r_new, norms), add_limbs(r_new * w_new, curves))

        sums = lax.fori_loop(0, 2, lambda i, v: update(i * (cx - 1), v), (no_faces, no_sums, no_sums))
        @pl.when(k < ITERS - 2)
        def _():
            halo_do(c, (0,), "start")

        sums = lax.fori_loop(1, cx - 1, update, sums)
        sz[c, 0], sz[c, 1] = sums[0]

        @pl.when(k < ITERS - 2)
        def _():
            halo_do(c, (1, 2), "start")

        send_sums(c, sums[1:])

        @pl.when(k < ITERS - 2)
        def _():
            apply(c)

        return gamma, alpha

    carry = lax.fori_loop(0, ITERS - 1, iteration, (jnp.full((1, 1), jnp.inf, jnp.float32), jnp.ones((1, 1), jnp.float32)))
    b = (ITERS - 1) % 2
    gamma, delta = wait_sums(b)
    alpha, beta = steps(gamma, delta, *carry)
    done_sums(b)

    def finish(x, carry):
        s_new = ext[b, x + 1] + beta * s[x]
        r_old = ext[START, x + 1]
        pressure[x] = pressure[x] + alpha * (r_old + beta * p[x])
        residual[x] = r_old - alpha * s_new
        return carry

    lax.fori_loop(0, cx, finish, 0)


def solution(mesh):
    counts = tuple(mesh.shape[a] for a in AXES)
    total = counts[0] * counts[1] * counts[2]

    def on_device(right_side, cell_type, relax_weight):
        cx, cy, cz = right_side.shape
        field = pltpu.VMEM((cx, cy, cz), jnp.float32)
        out = jax.ShapeDtypeStruct(right_side.shape, jnp.float32)
        vmem = pl.BlockSpec(memory_space=pltpu.VMEM)
        return pl.pallas_call(
            functools.partial(kernel, counts),
            out_shape=(out, out),
            in_specs=[vmem] * 3,
            out_specs=(vmem, vmem),
            scratch_shapes=[
                pltpu.VMEM((4, cx + 2, cy, cz), jnp.float32),
                pltpu.VMEM((4, 2, cx, cz), jnp.float32),
                pltpu.VMEM((4, 2, ROWS, LANES), jnp.float32),
                pltpu.VMEM((4, 2, cx, cz), jnp.float32),
                pltpu.VMEM((4, 2, ROWS, LANES), jnp.float32),
                field, field, field, field, field, field,
                pltpu.VMEM((2, 1, LANES), jnp.int32),
                pltpu.VMEM((2, total, LANES), jnp.int32),
                pltpu.SemaphoreType.DMA((4, 6)),
                pltpu.SemaphoreType.DMA((4, 6)),
                pltpu.SemaphoreType.DMA((2, total - 1)),
                pltpu.SemaphoreType.DMA((2, total - 1)),
            ],
            compiler_params=pltpu.CompilerParams(collective_id=0, has_side_effects=True),
        )(right_side, cell_type, relax_weight)

    spec = P(*AXES)
    return jax.shard_map(
        on_device, mesh=mesh, in_specs=(spec, spec, spec), out_specs=(spec, spec), check_vma=False)
```

time: 784 us -> 80.9 us (0.10); the launches traced: 771 us -> 80.7 us
  blocking collectives: 241 us -> 0 us
  starting transfers between devices: 139 us -> 0 us
  between operations: 133 us -> 0.65 us
  other arithmetic: 125 us -> 0 us
  local copies, waits for them, and re-layouts: 85.7 us -> 3.36 us
  Pallas kernels: 0 us -> 76.7 us
  waiting for transfers between devices: 46.8 us -> 0 us
    psum x45 -> x0, blocking collectives: 241 us -> none  [the longest x15 112 us: global_sums(): summed = lax.psum(second, 'gz')]
    ppermute x54 -> x0, starting transfers between devices: 139 us -> none  [the longest x27 104 us: extended(): lax.ppermute(tail, axis, [(i, (i + 1) % count) for i in range(ends)])]
    pallas_call x0 -> x1, Pallas kernels: none -> 76.7 us  [on_device(): pl.pallas_call(functools.partial(kernel, counts), out_shape=(out, out), i...]
    mul x8 -> x0, other arithmetic: 58.9 us -> none  [local_limbs(): limbs = split_limbs(first * second)]
    slice x69 -> x0, local copies, waits for them, and re-layouts: 52.4 us -> none  [the longest x26 23.5 us: extended(): head = lax.slice_in_dim(cells, 0, width, axis=dim)]
    ppermute x54 -> x0, waiting for transfers between devices: 46.8 us -> none  [the longest x27 36.2 us: extended(): lax.ppermute(head, axis, [((i + 1) % count, i) for i in range(ends)])]
    reduce_sum x16 -> x0, other arithmetic: 44.6 us -> none  [local_limbs(): return normalize([jnp.sum(limb, dtype=jnp.int32) for limb in limbs])]
    ppermute x36 -> x0, local copies, waits for them, and re-layouts: 31.9 us -> none  [the longest x18 16.3 us: extended(): lax.ppermute(head, axis, [((i + 1) % count, i) for i in range(ends)])]
  transfers between devices with their start and end apart: 54 -> 0, of which waited for: 26 -> 0; matrix products, arithmetic and copies ran while one was open for 5% -> 0% of each run, Pallas kernels for 0% -> 0%
where the time goes in v1:
time: 80.9 us; the launch traced here: 80.7 us
  Pallas kernels  76.7 us (95%)
  local copies, waits for them, and re-layouts  3.36 us (4%)
    pallas_call x1, Pallas kernels, on_device(): pl.pallas_call(functools.partial(kernel, counts), out_shape=(out, out), i...  76.7 us
    unnamed x4, local copies, waits for them, and re-layouts  3.36 us

profile of v1, /device:TPU:0, one launch (start us, length us, event | category | flops | bytes accessed | tf_op | source)
XLA Modules:
  0.0 80.7 jit_solution(16102421479098318247)
XLA Ops:
  0.6 76.7 %shard_map.50 = (f32[16,64,256]{2,1,0:T(8,128)}, f32[16,64,256]{2,1,0:T(8,128)}) custom-call(f32[16,64,256]{2,1,0:T(8,128)} %rhs.1, s32[16,64,256]{2,1,0:T(8,128)} %kind.1, f32[16,64,256]{2,1,0:T(8,128)} %relax.1), custom_call_target="tpu_custom_call" | custom-call | tf_op jit(solution)/shard_map/pallas_call | solution.py:300
  77.3 0.0 copy-start
  77.4 2.4 %copy.7 = f32[16,64,256]{2,1,0:T(8,128)} copy(f32[16,64,256]{2,1,0:T(8,128)} %get-tuple-element.4) | data formatting | bytes 2097152
  79.7 0.0 copy-done
  79.7 1.0 %copy.8 = f32[16,64,256]{2,1,0:T(8,128)} copy(f32[16,64,256]{2,1,0:T(8,128)S(1)} %copy-done) | data formatting | bytes 2097152
Async XLA Ops:
  77.3 2.4 %copy-start = (f32[16,64,256]{2,1,0:T(8,128)S(1)}, f32[16,64,256]{2,1,0:T(8,128)}, u32[]{:S(2)}) copy-start(f32[16,64,256]{2,1,0:T(8,128)} %get-tuple-element.5) | copy-start | bytes 3145732

commit v2 on v1

--- a/solution.py
+++ b/solution.py
@@ -15,7 +15,7 @@
 OPEN, START = 2, 3
 
 
-def kernel(counts, rhs, kind, relax, pressure, residual, ext, hy, hz, sy, sz, p, s, z, n, weight, fluid,
+def kernel(counts, rhs_in, kind_in, relax_in, pressure_out, residual_out, rhs, kind, relax, pressure, residual, io, ext, hy, hz, sy, sz, p, s, z, n, weight, fluid,
            mine, others, hsend, hrecv, asend, arecv):
     cx, cy, cz = rhs.shape
     tiles = cy // ROWS
@@ -31,6 +31,10 @@
     def peer(o):
         return tuple(lax.rem(m + v, c) if v else m for m, v, c in zip(me, o, counts))
 
+    loads = [pltpu.make_async_copy(src, dst, io.at[i])
+             for i, (src, dst) in enumerate(((kind_in, kind), (rhs_in, rhs), (relax_in, relax)))]
+    for load in loads:
+        load.start()
     barrier = pltpu.get_barrier_semaphore()
 
     def halo(b, axis, up):
@@ -122,8 +126,7 @@
                     v = v & 4095
                 rows.append(jnp.sum(v, axis=0, keepdims=True))
         block = jnp.concatenate(rows, 0)
-        for shift in (64, 32, 16, 8, 4, 2, 1):
-            block = block + pltpu.roll(block, shift, 1)
+        block = jnp.sum(block, axis=1, keepdims=True)
         diag = lane == lax.broadcasted_iota(jnp.int32, (ROWS, LANES), 0)
         mine[k] = jnp.sum(jnp.where(diag, block, 0), axis=0, keepdims=True)
         for i, o in enumerate(offsets):
@@ -178,6 +181,8 @@
         ext[START, x + 1] = start
         return pack_faces(OPEN, x, is_open, packed_open), pack_faces(START, x, start, packed_start)
 
+    for load in loads:
+        load.wait()
     packed_open, packed_start = lax.fori_loop(0, cx, first, (no_faces, no_faces))
     for b, packed in ((OPEN, packed_open), (START, packed_start)):
         sz[b, 0], sz[b, 1] = packed
@@ -218,10 +223,15 @@
             n[x] = weight[x] * centre - fluid[x] * around
             return carry
 
+        def pair(i, carry):
+            return one(2 * i + 2, one(2 * i + 1, carry))
+
         halo_do(b, (1, 2), "recv")
-        lax.fori_loop(1, cx - 1, one, 0)
+        lax.fori_loop(0, (cx - 2) // 2, pair, 0)
+        if cx % 2:
+            one(cx - 2, 0)
         halo_do(b, (0,), "recv")
-        lax.fori_loop(0, 2, lambda i, c: one(i * (cx - 1), c), 0)
+        one(cx - 1, one(0, 0))
 
     apply(0)
     for b in (OPEN, START):
@@ -237,22 +247,20 @@
 
         def update(x, carry):
             packed, norms, curves = carry
-            old = ext[b, x + 1]
             z_new = n[x] + beta * z[x]
             z[x] = z_new
-            w_new = old - alpha * z_new
+            w_old = ext[b, x + 1]
+            s_new = w_old + beta * s[x]
+            s[x] = s_new
+            w_new = w_old - alpha * z_new
             ext[c, x + 1] = w_new
-            s_new = old + beta * s[x]
-            s[x] = s_new
-            r_old = ext[START, x + 1]
-            p_new = r_old + beta * p[x]
-            p[x] = p_new
-            pressure[x] = pressure[x] + alpha * p_new
+            r_old = ext[START + b, x + 1]
             r_new = r_old - alpha * s_new
-            ext[START, x + 1] = r_new
+            ext[START + c, x + 1] = r_new
             return (pack_faces(c, x, w_new, packed), add_limbs(r_new * r_new, norms), add_limbs(r_new * w_new, curves))
 
         sums = lax.fori_loop(0, 2, lambda i, v: update(i * (cx - 1), v), (no_faces, no_sums, no_sums))
+
         @pl.when(k < ITERS - 2)
         def _():
             halo_do(c, (0,), "start")
@@ -265,6 +273,14 @@
             halo_do(c, (1, 2), "start")
 
         send_sums(c, sums[1:])
+
+        def follow(x, carry):
+            p_new = ext[START + b, x + 1] + beta * p[x]
+            p[x] = p_new
+            pressure[x] = pressure[x] + alpha * p_new
+            return carry
+
+        lax.fori_loop(0, cx, follow, 0)
 
         @pl.when(k < ITERS - 2)
         def _():
@@ -280,12 +296,22 @@
 
     def finish(x, carry):
         s_new = ext[b, x + 1] + beta * s[x]
-        r_old = ext[START, x + 1]
+        r_old = ext[START + b, x + 1]
         pressure[x] = pressure[x] + alpha * (r_old + beta * p[x])
         residual[x] = r_old - alpha * s_new
         return carry
 
-    lax.fori_loop(0, cx, finish, 0)
+    stores = []
+    parts = next(m for m in (4, 2, 1) if cx % m == 0)
+    for i in range(parts):
+        size = cx // parts
+        lax.fori_loop(i * size, (i + 1) * size, finish, 0)
+        for j, (src, dst) in enumerate(((pressure, pressure_out), (residual, residual_out))):
+            where = pl.ds(i * size, size)
+            stores.append(pltpu.make_async_copy(src.at[where], dst.at[where], io.at[3 + 2 * i + j]))
+            stores[-1].start()
+    for store in stores:
+        store.wait()
 
 
 def solution(mesh):
@@ -296,14 +322,16 @@
         cx, cy, cz = right_side.shape
         field = pltpu.VMEM((cx, cy, cz), jnp.float32)
         out = jax.ShapeDtypeStruct(right_side.shape, jnp.float32)
-        vmem = pl.BlockSpec(memory_space=pltpu.VMEM)
+        whole = pl.BlockSpec(memory_space=pl.ANY)
         return pl.pallas_call(
             functools.partial(kernel, counts),
             out_shape=(out, out),
-            in_specs=[vmem] * 3,
-            out_specs=(vmem, vmem),
+            in_specs=[whole] * 3,
+            out_specs=(whole, whole),
             scratch_shapes=[
-                pltpu.VMEM((4, cx + 2, cy, cz), jnp.float32),
+                field, pltpu.VMEM((cx, cy, cz), jnp.int32), field, field, field,
+                pltpu.SemaphoreType.DMA((11,)),
+                pltpu.VMEM((5, cx + 2, cy, cz), jnp.float32),
                 pltpu.VMEM((4, 2, cx, cz), jnp.float32),
                 pltpu.VMEM((4, 2, ROWS, LANES), jnp.float32),
                 pltpu.VMEM((4, 2, cx, cz), jnp.float32),

time: 80.9 us -> 74.6 us (0.922)
  Pallas kernels: 76.7 us -> 70.5 us
    pallas_call x1, Pallas kernels: 76.7 us -> 70.5 us  [on_device(): pl.pallas_call(functools.partial(kernel, counts), out_shape=(out, out), i...]
where the time goes in v2:
time: 74.6 us; the launch traced here: 74.5 us
  Pallas kernels  70.5 us (95%)
  local copies, waits for them, and re-layouts  3.36 us (5%)
    pallas_call x1, Pallas kernels, on_device(): pl.pallas_call(functools.partial(kernel, counts), out_shape=(out, out), i...  70.5 us
    unnamed x4, local copies, waits for them, and re-layouts  3.36 us

profile of v2, /device:TPU:0, one launch (start us, length us, event | category | flops | bytes accessed | tf_op | source)
XLA Modules:
  0.0 74.5 jit_solution(13998432934670855579)
XLA Ops:
  0.6 70.5 %shard_map.50 = (f32[16,64,256]{2,1,0:T(8,128)}, f32[16,64,256]{2,1,0:T(8,128)}) custom-call(f32[16,64,256]{2,1,0:T(8,128)} %rhs_in.1, s32[16,64,256]{2,1,0:T(8,128)} %kind_in.1, f32[16,64,256]{2,1,0:T(8,128)} %relax_in.1), custom_call_target="tpu_custom_call" | custom-call | tf_op jit(solution)/shard_map/pallas_call | solution.py:326
  71.1 0.0 copy-start
  71.1 2.4 %copy.7 = f32[16,64,256]{2,1,0:T(8,128)} copy(f32[16,64,256]{2,1,0:T(8,128)} %get-tuple-element.4) | data formatting | bytes 2097152
  73.5 0.0 copy-done
  73.5 1.0 %copy.8 = f32[16,64,256]{2,1,0:T(8,128)} copy(f32[16,64,256]{2,1,0:T(8,128)S(1)} %copy-done) | data formatting | bytes 2097152
Async XLA Ops:
  71.1 2.4 %copy-start = (f32[16,64,256]{2,1,0:T(8,128)S(1)}, f32[16,64,256]{2,1,0:T(8,128)}, u32[]{:S(2)}) copy-start(f32[16,64,256]{2,1,0:T(8,128)} %get-tuple-element.5) | copy-start | bytes 3145732

commit v3 on v2

--- a/solution.py
+++ b/solution.py
@@ -268,11 +268,11 @@
         sums = lax.fori_loop(1, cx - 1, update, sums)
         sz[c, 0], sz[c, 1] = sums[0]
 
+        send_sums(c, sums[1:])
+
         @pl.when(k < ITERS - 2)
         def _():
             halo_do(c, (1, 2), "start")
-
-        send_sums(c, sums[1:])
 
         def follow(x, carry):
             p_new = ext[START + b, x + 1] + beta * p[x]

time: 74.6 us -> 74.7 us (level)
  no operation moved by 1% of the time
where the time goes in v3:
time: 74.7 us; the launch traced here: 74.5 us
  Pallas kernels  70.5 us (94%)
  local copies, waits for them, and re-layouts  3.36 us (4%)
    pallas_call x1, Pallas kernels, on_device(): pl.pallas_call(functools.partial(kernel, counts), out_shape=(out, out), i...  70.5 us
    unnamed x4, local copies, waits for them, and re-layouts  3.36 us

profile of v3, /device:TPU:0, one launch (start us, length us, event | category | flops | bytes accessed | tf_op | source)
XLA Modules:
  0.0 74.5 jit_solution(5630677309009184761)
XLA Ops:
  0.6 70.5 %shard_map.50 = (f32[16,64,256]{2,1,0:T(8,128)}, f32[16,64,256]{2,1,0:T(8,128)}) custom-call(f32[16,64,256]{2,1,0:T(8,128)} %rhs_in.1, s32[16,64,256]{2,1,0:T(8,128)} %kind_in.1, f32[16,64,256]{2,1,0:T(8,128)} %relax_in.1), custom_call_target="tpu_custom_call" | custom-call | tf_op jit(solution)/shard_map/pallas_call | solution.py:326
  71.2 0.0 copy-start
  71.2 2.4 %copy.7 = f32[16,64,256]{2,1,0:T(8,128)} copy(f32[16,64,256]{2,1,0:T(8,128)} %get-tuple-element.4) | data formatting | bytes 2097152
  73.6 0.0 copy-done
  73.6 1.0 %copy.8 = f32[16,64,256]{2,1,0:T(8,128)} copy(f32[16,64,256]{2,1,0:T(8,128)S(1)} %copy-done) | data formatting | bytes 2097152
Async XLA Ops:
  71.2 2.4 %copy-start = (f32[16,64,256]{2,1,0:T(8,128)S(1)}, f32[16,64,256]{2,1,0:T(8,128)}, u32[]{:S(2)}) copy-start(f32[16,64,256]{2,1,0:T(8,128)} %get-tuple-element.5) | copy-start | bytes 3145732
